TPU v7x, 32 devices: a whole 2x2x4 slice. The times are simulated.
32 devices in a mesh: dp: 4 (over x, core), ctx: 8 (over z, y).
Axes of the slice: x: 2, y: 2, z: 4, core: 2. Of those that a mesh axis runs over, the one named last changes fastest.
Arguments:
- tokens: bfloat16 [4096, 1792], P(('dp', 'ctx')), may hold values from -6 to 6
- cotangent: bfloat16 [4096, 1792], P(('dp', 'ctx')), may hold values from -6 to 6
- expert_ids: int32 [4096, 4], P(('dp', 'ctx')), may hold values from 0 to 15, all different within a row; in each aligned block of 128 rows (0 to 127, 128 to 255, ...) at most 40 rows name the same one
- norm_gain: float32 [1792], replicated, may hold values from 0.5 to 1.5
- router_weight: bfloat16 [1792, 16], replicated, may hold values from -0.125 to 0.125
- gate_weight: bfloat16 [16, 1792, 1536], P('ctx', None, 'dp'), may hold values from -0.125 to 0.125
- up_weight: bfloat16 [16, 1792, 1536], P('ctx', None, 'dp'), may hold values from -0.125 to 0.125
- down_weight: bfloat16 [16, 1536, 1792], P('ctx', 'dp'), may hold values from -0.15625 to 0.15625
Outputs:
- grad_tokens: bfloat16 [4096, 1792], P(('dp', 'ctx'))
- grad_gate: bfloat16 [16, 1792, 1536], P('ctx', None, 'dp')
- grad_up: bfloat16 [16, 1792, 1536], P('ctx', None, 'dp')
- grad_down: bfloat16 [16, 1536, 1792], P('ctx', 'dp')
- grad_router: float32 [1792, 16], P(('dp', 'ctx'))
- grad_gain: float32 [1792], P(('dp', 'ctx'))
Inputs may be any that keep to these rules, and one draw needn't show every extreme that they name: `expert_ids`: each row names 4 different experts; among the rows of one device no expert is named more than 40 times.
All inputs are finite; a program needn't handle non-finite values.
Results may differ from a plain program's by a relative error of at most 0.02.
Values may be sent and summed in bfloat16 or wider, within the bound.
No kernel may reach another device: no remote copies, remote signals or barrier semaphores. Data moves between devices by JAX's collectives and lax.ppermute only.
A program may use at most 192 MiB of HBM per device.

v0:
```python
import jax
import jax.numpy as jnp
from jax import lax
from jax.sharding import PartitionSpec as P

EPSILON = 1e-05
SWISH_SCALE = 1.702


def expert_pass(rows, upstream, weight, gate_weight, up_weight, down_weight):
    gate_pre = jnp.einsum("prd,pdf->prf", rows, gate_weight, preferred_element_type=jnp.float32)
    up_pre = jnp.einsum("prd,pdf->prf", rows, up_weight, preferred_element_type=jnp.float32)
    squash = jax.nn.sigmoid(SWISH_SCALE * gate_pre)
    hidden = (gate_pre * squash * (up_pre + 1.0)).astype(jnp.bfloat16)
    grad_out = jnp.einsum("prd,pfd->prf", upstream, down_weight, preferred_element_type=jnp.float32)
    score = jnp.sum(grad_out * hidden.astype(jnp.float32), axis=2)
    grad_hidden = weight[:, :, None] * grad_out
    slope = squash + SWISH_SCALE * gate_pre * squash * (1.0 - squash)
    grad_pre_gate = (grad_hidden * (up_pre + 1.0) * slope).astype(jnp.bfloat16)
    grad_pre_up = (grad_hidden * gate_pre * squash).astype(jnp.bfloat16)
    scaled_up = (weight[:, :, None] * upstream.astype(jnp.float32)).astype(jnp.bfloat16)
    down_grad = jnp.einsum(
        "prf,prd->pfd", hidden, scaled_up, preferred_element_type=jnp.float32
    ).astype(jnp.bfloat16)
    gate_grad = jnp.einsum(
        "prd,prf->pdf", rows, grad_pre_gate, preferred_element_type=jnp.float32
    ).astype(jnp.bfloat16)
    up_grad = jnp.einsum(
        "prd,prf->pdf", rows, grad_pre_up, preferred_element_type=jnp.float32
    ).astype(jnp.bfloat16)
    back = jnp.einsum(
        "prf,pdf->prd", grad_pre_gate, gate_weight, preferred_element_type=jnp.float32
    )
    back = back + jnp.einsum(
        "prf,pdf->prd", grad_pre_up, up_weight, preferred_element_type=jnp.float32
    )
    return (gate_grad, up_grad, down_grad, back, score)


def body(
    tokens, cotangent, expert_ids, norm_gain, router_weight, gate_weight, up_weight, down_weight
):
    ctx_size = lax.axis_size("ctx")
    local = gate_weight.shape[0]
    experts = router_weight.shape[1]
    rows_here = tokens.shape[0]
    picks = expert_ids.shape[1]
    width = tokens.shape[1]
    assigned = rows_here * picks
    capacity = max(2, rows_here * picks * 5 // (4 * experts))
    slots = experts * capacity
    widened = tokens.astype(jnp.float32)
    inverse = lax.rsqrt(jnp.mean(widened * widened, axis=1, keepdims=True) + EPSILON)
    scaled = widened * inverse
    normed = (scaled * norm_gain).astype(jnp.bfloat16)
    logits = jnp.dot(normed, router_weight, preferred_element_type=jnp.float32)
    labels = jnp.arange(experts, dtype=jnp.int32)
    member = expert_ids[:, :, None] == labels
    chosen = jnp.sum(jnp.where(member, logits[:, None, :], 0.0), axis=2)
    lifted = jnp.exp(chosen)
    gates = lifted / jnp.sum(lifted, axis=1, keepdims=True)
    hits = member.reshape(assigned, experts).astype(jnp.int32)
    rank = jnp.sum((jnp.cumsum(hits, axis=0) - 1) * hits, axis=1)
    position = expert_ids.reshape(-1) * capacity + rank
    match = (jnp.arange(slots, dtype=jnp.int32)[:, None] == position[None, :]).astype(jnp.float32)
    dispatch = jnp.sum(match.reshape(slots, rows_here, picks), axis=2)
    dispatch_low = dispatch.astype(jnp.bfloat16)
    out_rows = jnp.dot(dispatch_low, normed, preferred_element_type=jnp.float32).astype(
        jnp.bfloat16
    )
    out_rows = out_rows.reshape(ctx_size, local, capacity, width)
    out_grad = jnp.dot(dispatch_low, cotangent, preferred_element_type=jnp.float32).astype(
        jnp.bfloat16
    )
    out_grad = out_grad.reshape(ctx_size, local, capacity, width)
    out_gate = jnp.dot(match, gates.reshape(-1), precision=lax.Precision.HIGHEST)
    out_gate = out_gate.reshape(ctx_size, local, capacity)
    arrived = (
        lax.all_to_all(out_rows, "ctx", split_axis=0, concat_axis=2, tiled=True),
        lax.all_to_all(out_grad, "ctx", split_axis=0, concat_axis=2, tiled=True),
        lax.all_to_all(
            out_gate.astype(jnp.bfloat16), "ctx", split_axis=0, concat_axis=2, tiled=True
        ).astype(out_gate.dtype),
    )
    rows, upstream, weight = (
        lax.all_gather(arrived[0], "dp", axis=2, tiled=True),
        lax.all_gather(arrived[1], "dp", axis=2, tiled=True),
        lax.all_gather(arrived[2].astype(jnp.bfloat16), "dp", axis=2, tiled=True).astype(
            jnp.float32
        ),
    )
    gate_grad, up_grad, down_grad, back, score = expert_pass(
        rows[0], upstream[0], weight[0], gate_weight, up_weight, down_weight
    )
    back_mine, score_mine = (
        lax.psum_scatter(back.astype(jnp.bfloat16), "dp", scatter_dimension=1, tiled=True).astype(
            jnp.float32
        ),
        lax.psum_scatter(score.astype(jnp.bfloat16), "dp", scatter_dimension=1, tiled=True).astype(
            jnp.float32
        ),
    )
    back_slots, score_slots = (
        lax.all_to_all(
            back_mine.astype(jnp.bfloat16), "ctx", split_axis=1, concat_axis=0, tiled=True
        ).astype(back_mine.dtype),
        lax.all_to_all(
            score_mine.astype(jnp.bfloat16), "ctx", split_axis=1, concat_axis=0, tiled=True
        ).astype(score_mine.dtype),
    )
    back_flat = back_slots.reshape(slots, width)
    score_flat = score_slots.reshape(slots)
    grad_tok = jnp.dot(dispatch.T, back_flat, precision=lax.Precision.HIGHEST)
    score_tok = jnp.dot(score_flat, match, precision=lax.Precision.HIGHEST).reshape(
        rows_here, picks
    )
    mixed = jnp.sum(gates * score_tok, axis=1, keepdims=True)
    grad_chosen = gates * (score_tok - mixed)
    grad_logits = jnp.sum(jnp.where(member, grad_chosen[:, :, None], 0.0), axis=1).astype(
        jnp.bfloat16
    )
    grad_normed = grad_tok + jnp.dot(
        grad_logits, router_weight.T, preferred_element_type=jnp.float32
    )
    router_part = jnp.dot(normed.T, grad_logits, preferred_element_type=jnp.float32)
    gain_part = jnp.sum(grad_normed * scaled, axis=0)
    router_grad, gain_grad = (
        lax.psum_scatter(router_part, ("dp", "ctx"), scatter_dimension=0, tiled=True),
        lax.psum_scatter(gain_part, ("dp", "ctx"), scatter_dimension=0, tiled=True),
    )
    grad_scaled = grad_normed * norm_gain
    correction = jnp.mean(grad_scaled * scaled, axis=1, keepdims=True)
    grad_input = (
        cotangent.astype(jnp.float32) + inverse * (grad_scaled - scaled * correction)
    ).astype(jnp.bfloat16)
    return (grad_input, gate_grad, up_grad, down_grad, router_grad, gain_grad)


def solution(mesh):
    return jax.shard_map(
        body,
        mesh=mesh,
        in_specs=(
            P(("dp", "ctx"), None),
            P(("dp", "ctx"), None),
            P(("dp", "ctx"), None),
            P(),
            P(),
            P("ctx", None, "dp"),
            P("ctx", None, "dp"),
            P("ctx", "dp", None),
        ),
        out_specs=(
            P(("dp", "ctx"), None),
            P("ctx", None, "dp"),
            P("ctx", None, "dp"),
            P("ctx", "dp", None),
            P(("dp", "ctx"), None),
            P(("dp", "ctx")),
        ),
        check_vma=False,
    )
```

profile of v0, /device:TPU:0, one launch (start us, length us, event | category | flops | bytes accessed | tf_op | source)
XLA Modules:
  0.0 604.0 jit_solution(15963162471281344825)
XLA Ops:
  7.2 0.9 copy.135
  8.4 1.2 fusion.36
  9.6 1.2 reduce-window.6
  12.2 1.8 convolution_convert_fusion
  14.0 59.6 %all_to_all.85 = bf16[8,2,40,1792]{3,2,1,0:T(8,128)(2,1)S(1)} all-to-all(bf16[8,2,40,1792]{3,2,1,0:T(8,128)(2,1)S(1)} %bitcast.98), channel_id=1, replica_groups=mesh['dp'=4,'ctx'=8] {'ctx'}, dimensions={0} | all-to-all | bytes 4587520 | tf_op jit(solution)/shard_map/all_to_all | solution.py:79
  73.7 1.5 copy.144
  76.0 55.6 %all_to_all.86 = bf16[8,2,40,1792]{3,2,1,0:T(8,128)(2,1)S(1)} all-to-all(bf16[8,2,40,1792]{3,2,1,0:T(8,128)(2,1)S(1)} %bitcast.99), channel_id=1, replica_groups=mesh['dp'=4,'ctx'=8] {'ctx'}, dimensions={0} | all-to-all | bytes 4587520 | tf_op jit(solution)/shard_map/all_to_all | solution.py:80
  131.7 1.5 copy.143
  133.8 1.1 fusion.50
  136.8 1.0 iota_compare_fusion
  137.8 9.5 %fusion.5 = f32[2,1280,384]{1,2,0:T(8,128)} fusion(bf16[2,1792,384]{2,1,0:T(8,128)(2,1)S(1)} %copy-done, bf16[1,2,1280,1792]{3,2,1,0:T(8,128)(2,1)} %all-gather.5.cloned.1.call-done), kind=kOutput, calls=%fused_computation.7 | convolution fusion | flops 3523215360 | bytes 15859712 | tf_op jit(solution)/shard_map/prd,pdf->prf/dot_general | solution.py:11
  147.3 11.2 %fusion.13 = f32[2,1280,384]{1,2,0:T(8,128)} fusion(bf16[2,1792,384]{2,1,0:T(8,128)(2,1)S(1)} %copy-done.6, bf16[1,2,1280,1792]{3,2,1,0:T(8,128)(2,1)} %all-gather.5.cloned.1.call-done), kind=kOutput, calls=%fused_computation.15 | convolution fusion | flops 3524198400 | bytes 15859712 | tf_op jit(solution)/shard_map/prd,pdf->prf/dot_general | solution.py:12
  158.5 43.5 %all-gather.3.cloned.1.call-done = bf16[1,2,1280,1792]{3,2,1,0:T(8,128)(2,1)} async-done(((bf16[1,2,320,1792]{3,2,1,0:T(8,128)(2,1)}), bf16[1,2,1280,1792]{3,2,1,0:T(8,128)(2,1)}) %all-gather.3.cloned.1.call-update) | async-done | bytes 9175056 | tf_op jit(solution)/shard_map/all_gather | solution.py:87
  201.9 13.7 %multiply_reduce_fusion = (bf16[2,1280]{1,0:T(2,128)(2,1)}, bf16[2,1280,384]{1,2,0:T(8,128)(2,1)}, f32[2,1280,384]{1,2,0:T(8,128)}) fusion(f32[2,1280,384]{1,2,0:T(8,128)} %fusion.13, f32[2,1280,384]{1,2,0:T(8,128)} %fusion.5, bf16[2,384,1792]{2,1,0:T(8,128)(2,1)} %param.15, bf16[1,2,1280,1792]{3,2,1,0:T(8,128)(2,1)} %all-gather.3.cloned.1.call-done), kind=kOutput, calls=%fused_computation.16 | convolution fusion | flops 3533043200 | bytes 25695232 | tf_op jit(solution)/shard_map/prd,pfd->prf/dot_general | solution.py:15
  215.7 1.6 copy.173
  217.9 20.0 %reduce-scatter.8.cloned.1.call-done = bf16[320,2]{1,0:T(8,128)(2,1)} async-done(((bf16[1280,2]{1,0:T(8,128)(2,1)}), bf16[320,2]{1,0:T(8,128)(2,1)}) %reduce-scatter.8.cloned.1.call-update) | async-done | bytes 1296
  237.9 1.6 copy.152
  239.5 5.5 all-to-all-start.4
  245.8 2.1 eq.110
  247.9 3.6 all-to-all-done.4
  252.3 2.1 select_reduce_fusion
  254.4 0.9 copy.168
  255.3 1.9 multiply_reduce_fusion.1
  257.2 1.4 copy.139
  258.6 1.5 reshape.149
  260.1 1.9 fusion.23
  262.0 8.9 %all_to_all.87 = bf16[8,2,40]{2,1,0:T(2,128)(2,1)S(1)} all-to-all(bf16[8,2,40]{2,1,0:T(2,128)(2,1)S(1)} %convert_element_type.83), channel_id=1, replica_groups=mesh['dp'=4,'ctx'=8] {'ctx'}, dimensions={0} | all-to-all | bytes 2560 | tf_op jit(solution)/shard_map/all_to_all | solution.py:81
  271.5 1.3 all_to_all.65
  272.9 1.5 copy.141
  274.4 7.1 %all_gather.9 = bf16[1,2,1280]{1,0,2:T(2,128)(2,1)S(1)} all-gather(bf16[1,2,320]{1,0,2:T(2,128)(2,1)} %copy.141), channel_id=1, replica_groups=mesh['dp'=4,'ctx'=8] {'dp'}, dimensions={2}, use_global_device_ids=true | all-gather | bytes 6400 | tf_op jit(solution)/shard_map/all_gather | solution.py:88
  281.5 1.4 mul.155
  282.9 1.9 copy.142
  284.8 6.4 %multiply_convert_fusion.3 = (bf16[2,1280,384]{1,2,0:T(8,128)(2,1)}, bf16[2,1280,384]{1,2,0:T(8,128)(2,1)S(1)}) fusion(f32[2,1280,384]{1,2,0:T(8,128)} %fusion.5, f32[2,1280,384]{1,2,0:T(8,128)} %get-tuple-element.14, f32[2,1280]{1,0:T(2,128)} %copy.142, f32[2,1280,384]{1,2,0:T(8,128)} %fusion.13), kind=kLoop, calls=%fused_computation.18 | loop fusion | flops 14745600 | bytes 15738880 | tf_op jit(solution)/shard_map/convert_element_type | solution.py:20
  291.3 9.3 %fusion.52 = f32[2,1280,1792]{2,1,0:T(8,128)} fusion(bf16[2,1280,384]{1,2,0:T(8,128)(2,1)S(1)} %get-tuple-element.13, bf16[2,1792,384]{2,1,0:T(8,128)(2,1)S(1)} %copy-done), kind=kOutput, calls=%fused_computation.77 | convolution fusion | flops 3523215360 | bytes 23068672 | tf_op jit(solution)/shard_map/prf,pdf->prd/dot_general | solution.py:31
  300.6 16.4 %add_convert_fusion = bf16[2,1280,1792]{2,1,0:T(8,128)(2,1)} fusion(f32[2,1280,1792]{2,1,0:T(8,128)} %fusion.52, bf16[2,1280,384]{1,2,0:T(8,128)(2,1)} %get-tuple-element.12, bf16[2,1792,384]{2,1,0:T(8,128)(2,1)} %param.14), kind=kOutput, calls=%fused_computation.1 | convolution fusion | flops 3532390400 | bytes 32243712 | tf_op jit(solution)/shard_map/prf,pdf->prd/dot_general | solution.py:34
  317.1 73.6 %reduce-scatter.6.cloned.1.call-done = bf16[2,320,1792]{2,1,0:T(8,128)(2,1)} async-done(((bf16[2,1280,1792]{2,1,0:T(8,128)(2,1)}), bf16[2,320,1792]{2,1,0:T(8,128)(2,1)}) %reduce-scatter.6.cloned.1.call-update) | async-done | bytes 2293776 | tf_op jit(solution)/shard_map/reduce_scatter | solution.py:96
  390.7 5.4 copy.149
  396.1 5.5 all-to-all-start.3
  402.0 0.9 fusion.45
  403.0 12.0 %fusion.20 = bf16[2,1792,384]{2,1,0:T(8,128)(2,1)} fusion(bf16[2,1280,384]{1,2,0:T(8,128)(2,1)} %get-tuple-element.12, bf16[1,2,1280,1792]{3,2,1,0:T(8,128)(2,1)} %all-gather.5.cloned.1.call-done), kind=kOutput, calls=%fused_computation.23 | convolution fusion | flops 3524591616 | bytes 13893632 | tf_op jit(solution)/shard_map/prd,prf->pdf/dot_general | solution.py:28
  415.0 9.7 %fusion.16 = bf16[2,384,1792]{2,1,0:T(8,128)(2,1)} fusion(bf16[2,1280,384]{1,2,0:T(8,128)(2,1)} %get-tuple-element.11, bf16[1,2,1280,1792]{3,2,1,0:T(8,128)(2,1)} %all-gather.3.cloned.1.call-done, f32[2,1280]{1,0:T(2,128)S(1)} %copy-done.10), kind=kOutput, calls=%fused_computation.21 | convolution fusion | flops 3538354176 | bytes 13903872 | tf_op jit(solution)/shard_map/prf,prd->pfd/dot_general | solution.py:22
  424.7 12.3 %fusion.17 = bf16[2,1792,384]{2,1,0:T(8,128)(2,1)} fusion(bf16[2,1280,384]{1,2,0:T(8,128)(2,1)S(1)} %copy-done.3, bf16[1,2,1280,1792]{3,2,1,0:T(8,128)(2,1)} %all-gather.5.cloned.1.call-done), kind=kOutput, calls=%fused_computation.22 | convolution fusion | flops 3524591616 | bytes 13893632 | tf_op jit(solution)/shard_map/prd,prf->pdf/dot_general | solution.py:25
  437.0 111.5 %all-reduce.4.cloned.1.call-done = f32[1792,16]{0,1:T(8,128)} async-done(((f32[1792,16]{0,1:T(8,128)}), f32[1792,16]{0,1:T(8,128)}) %all-reduce.4.cloned.1.call-update) | async-done | bytes 114704
  548.4 1.4 constant_dynamic-slice_fusion
  550.3 1.4 fusion.53
  551.7 1.4 fusion.35
  553.0 41.1 %all-reduce.1 = f32[1792]{0:T(1024)S(1)} all-reduce(f32[1792]{0:T(1024)S(1)} %get-tuple-element.6), channel_id=5, replica_groups=mesh['dp'=4,'ctx'=8] {'dp','ctx'}, use_global_device_ids=true, to_apply=%region_15.16.clone | all-reduce | flops 1792 | bytes 14336
  594.7 2.5 fusion.34
  (79 shorter events, 9.1 us)
Async XLA Ops:
  7.2 130.6 %copy-start = (bf16[2,1792,384]{2,1,0:T(8,128)(2,1)S(1)}, bf16[2,1792,384]{2,1,0:T(8,128)(2,1)}, u32[]{:S(2)}) copy-start(bf16[2,1792,384]{2,1,0:T(8,128)(2,1)} %param.13) | copy-start | bytes 8257540
  7.2 130.6 %all-gather.5.cloned.1.call-start = ((), (), s32[]{:S(2)}) async-start(), calls=%async_computation.8 | async-start | bytes 11468800 | tf_op jit(solution)/shard_map/all_gather | solution.py:86
  9.6 64.1 %copy-start.16 = (f32[128]{0:T(128)}, f32[128]{0:T(128)S(1)}, u32[]{:S(2)}) copy-start(f32[128]{0:T(128)S(1)} %add_rsqrt_fusion) | copy-start | bytes 1540
  11.1 2.9 copy-start.12
  73.7 1.6 copy-start.7
  75.2 126.7 %all-gather.3.cloned.1.call-start = ((), (), s32[]{:S(2)}) async-start(), calls=%async_computation.7 | async-start | bytes 11468800 | tf_op jit(solution)/shard_map/all_gather | solution.py:87
  131.6 2.1 copy-start.4
  131.6 2.1 copy-start.8
  131.7 3.3 copy-start.11
  133.2 104.7 %reduce-scatter.8.cloned.1.call-start = ((), (), s32[]{:S(2)}) async-start(), calls=%async_computation.10 | async-start | bytes 409600
  136.3 0.5 copy-start.15
  137.8 9.5 %copy-start.6 = (bf16[2,1792,384]{2,1,0:T(8,128)(2,1)S(1)}, bf16[2,1792,384]{2,1,0:T(8,128)(2,1)}, u32[]{:S(2)}) copy-start(bf16[2,1792,384]{2,1,0:T(8,128)(2,1)} %param.14) | copy-start | bytes 8257540
  158.5 86.8 %copy-start.14 = (f32[128,4]{0,1:T(4,128)S(1)}, f32[128,4]{0,1:T(4,128)}, u32[]{:S(2)}) copy-start(f32[128,4]{0,1:T(4,128)} %select_reduce_fusion.2) | copy-start | bytes 6148
  239.5 12.0 %all-to-all-start.4 = ((bf16[2,8,40]{2,0,1:T(2,128)(2,1)}), bf16[2,8,40]{2,0,1:T(2,128)(2,1)}, u32[]{:S(2)}, u32[]{:S(2)}) async-start(bf16[2,8,40]{2,0,1:T(2,128)(2,1)} %copy.152), calls=%async_computation.5 | async-start | bytes 8192 | tf_op jit(solution)/shard_map/all_to_all | solution.py:107
  245.0 145.7 %reduce-scatter.6.cloned.1.call-start = ((), (), s32[]{:S(2)}) async-start(), calls=%async_computation.9 | async-start | bytes 11468800 | tf_op jit(solution)/shard_map/reduce_scatter | solution.py:96
  291.3 9.4 %copy-start.2 = (bf16[2,1280,384]{1,2,0:T(8,128)(2,1)}, bf16[2,1280,384]{1,2,0:T(8,128)(2,1)S(1)}, u32[]{:S(2)}) copy-start(bf16[2,1280,384]{1,2,0:T(8,128)(2,1)S(1)} %get-tuple-element.13) | copy-start | bytes 5898244
  317.0 84.9 %copy-start.13 = (f32[128,4]{0,1:T(4,128)S(1)}, f32[128,4]{0,1:T(4,128)}, u32[]{:S(2)}) copy-start(f32[128,4]{0,1:T(4,128)} %get-tuple-element.9) | copy-start | bytes 6148
  317.1 84.9 %copy-start.19 = (f32[128]{0:T(128)S(1)}, f32[128]{0:T(128)}, u32[]{:S(2)}) copy-start(f32[128]{0:T(128)} %get-tuple-element.8) | copy-start | bytes 1540
  317.1 84.9 %copy-start.17 = (f32[128]{0:T(128)S(1)}, f32[128]{0:T(128)}, u32[]{:S(2)}) copy-start(f32[128]{0:T(128)} %copy-done.16) | copy-start | bytes 1540
  396.1 153.7 %all-to-all-start.3 = ((bf16[2,320,1792]{2,0,1:T(2,128)(2,1)}), bf16[2,320,1792]{2,0,1:T(2,128)(2,1)S(1)}, u32[]{:S(2)}, u32[]{:S(2)}) async-start(bf16[2,320,1792]{2,0,1:T(2,128)(2,1)} %copy.149), calls=%async_computation.4 | async-start | bytes 4587520 | tf_op jit(solution)/shard_map/all_to_all | solution.py:104
  401.6 146.8 %all-reduce.4.cloned.1.call-start = ((), (), s32[]{:S(2)}) async-start(), calls=%async_computation.11 | async-start | bytes 229376
  403.0 12.0 %copy-start.10 = (f32[2,1280]{1,0:T(2,128)S(1)}, f32[2,1280]{1,0:T(2,128)}, u32[]{:S(2)}) copy-start(f32[2,1280]{1,0:T(2,128)} %copy.142) | copy-start | bytes 30724
  415.0 9.7 %copy-start.3 = (bf16[2,1280,384]{1,2,0:T(8,128)(2,1)S(1)}, bf16[2,1280,384]{1,2,0:T(8,128)(2,1)}, u32[]{:S(2)}) copy-start(bf16[2,1280,384]{1,2,0:T(8,128)(2,1)} %copy-done.2) | copy-start | bytes 5898244
  550.0 1.6 copy-start.5
  550.1 1.6 copy-start.9
  550.1 1.6 copy-start.18
  550.2 46.9 %copy-start.1 = (bf16[2,1792,384]{2,1,0:T(8,128)(2,1)S(1)}, bf16[2,1792,384]{2,1,0:T(8,128)(2,1)}, u32[]{:S(2)}) copy-start(bf16[2,1792,384]{2,1,0:T(8,128)(2,1)} %param.13) | copy-start | bytes 8257540
Sparse Core Ops, SparseCore 0:
  75.3 61.6 all-gather.4
  139.2 62.7 all-gather.2
  217.4 20.4 reduce-scatter.7
  317.2 73.4 reduce-scatter.5
  408.3 140.1 all-reduce.3
where the time goes:
time: 608 us; the launch traced here: 604 us
  waiting for transfers between devices  252 us (41%)
  blocking collectives  172 us (28%)
  matrix products  103 us (17%)
  local copies, waits for them, and re-layouts  28.2 us (5%)
  other arithmetic  21.1 us (3%)
  between operations  14.4 us (2%)
  starting transfers between devices  12.2 us (2%)
    unnamed x7, waiting for transfers between devices  132 us
    reduce_scatter x1, waiting for transfers between devices, body(): lax.psum_scatter(back.astype(jnp.bfloat16), 'dp', scatter_dimension=1, ti...  73.6 us
    all_to_all x1, blocking collectives, body(): lax.all_to_all(out_rows, 'ctx', split_axis=0, concat_axis=2, tiled=True)  59.6 us
    all_to_all x1, blocking collectives, body(): lax.all_to_all(out_grad, 'ctx', split_axis=0, concat_axis=2, tiled=True)  55.6 us
    all_gather x1, waiting for transfers between devices, body(): lax.all_gather(arrived[1], 'dp', axis=2, tiled=True)  43.5 us
    unnamed x1, blocking collectives  41.1 us
    dot_general x1, matrix products, expert_pass(): jnp.einsum('prf,pdf->prd', grad_pre_up, up_weight, preferred_element_type...  16.4 us
    dot_general x1, matrix products, expert_pass(): jnp.einsum('prd,pfd->prf', upstream, down_weight, preferred_element_type=...  13.7 us
  transfers between devices with their start and end apart: 7, of which 5 were waited for; matrix products, arithmetic and copies ran while one was open for 11% of the time, Pallas kernels for 0%

commit v1 on v0

--- a/solution.py
+++ b/solution.py
@@ -77,7 +77,12 @@
     out_gate = out_gate.reshape(ctx_size, local, capacity)
     arrived = (
         lax.all_to_all(out_rows, "ctx", split_axis=0, concat_axis=2, tiled=True),
-        lax.all_to_all(out_grad, "ctx", split_axis=0, concat_axis=2, tiled=True),
+        jnp.concatenate(
+            lax.all_to_all(
+                jnp.stack(jnp.split(out_grad, lax.axis_size("ctx"), axis=0)), "ctx", 0, 0
+            ),
+            axis=2,
+        ),
         lax.all_to_all(
             out_gate.astype(jnp.bfloat16), "ctx", split_axis=0, concat_axis=2, tiled=True
         ).astype(out_gate.dtype),

time: 608 us -> 609 us (level)
  no operation moved by 1% of the time
where the time goes in v1:
time: 609 us; the launch traced here: 604 us
  waiting for transfers between devices  252 us (41%)
  blocking collectives  172 us (28%)
  matrix products  103 us (17%)
  local copies, waits for them, and re-layouts  28.9 us (5%)
  other arithmetic  21.1 us (3%)
  between operations  14.4 us (2%)
  starting transfers between devices  12.3 us (2%)
    unnamed x7, waiting for transfers between devices  132 us
    reduce_scatter x1, waiting for transfers between devices, body(): lax.psum_scatter(back.astype(jnp.bfloat16), 'dp', scatter_dimension=1, ti...  73.7 us
    all_to_all x1, blocking collectives, body(): lax.all_to_all(out_rows, 'ctx', split_axis=0, concat_axis=2, tiled=True)  59.6 us
    all_to_all x1, blocking collectives, body(): lax.all_to_all(jnp.stack(jnp.split(out_grad, lax.axis_size('ctx'), axis=0...  55.6 us
    all_gather x1, waiting for transfers between devices, body(): lax.all_gather(arrived[1], 'dp', axis=2, tiled=True)  43 us
    unnamed x1, blocking collectives  41.1 us
    dot_general x1, matrix products, expert_pass(): jnp.einsum('prf,pdf->prd', grad_pre_up, up_weight, preferred_element_type...  16.4 us
    dot_general x1, matrix products, expert_pass(): jnp.einsum('prd,pfd->prf', upstream, down_weight, preferred_element_type=...  13.7 us
  transfers between devices with their start and end apart: 7, of which 5 were waited for; matrix products, arithmetic and copies ran while one was open for 11% of the time, Pallas kernels for 0%

profile of v1, /device:TPU:0, one launch (start us, length us, event | category | flops | bytes accessed | tf_op | source)
XLA Modules:
  0.0 604.5 jit_solution(15081805893570523623)
XLA Ops:
  7.2 0.9 copy.135
  8.4 1.2 fusion.36
  9.6 1.2 reduce-window.6
  12.5 1.8 convolution_convert_fusion
  14.4 59.6 %all_to_all.72 = bf16[8,2,40,1792]{3,2,1,0:T(8,128)(2,1)S(1)} all-to-all(bf16[8,2,40,1792]{3,2,1,0:T(8,128)(2,1)S(1)} %bitcast.103), channel_id=1, replica_groups=mesh['dp'=4,'ctx'=8] {'ctx'}, dimensions={0} | all-to-all | bytes 4587520 | tf_op jit(solution)/shard_map/all_to_all | solution.py:79
  74.0 1.5 copy.144
  76.8 55.6 %all_to_all.73 = bf16[8,1,2,40,1792]{4,3,2,1,0:T(8,128)(2,1)S(1)} all-to-all(bf16[8,1,2,40,1792]{4,3,2,1,0:T(8,128)(2,1)S(1)} %constant_dynamic-update-slice_fusion), channel_id=1, replica_groups=mesh['dp'=4,'ctx'=8] {'ctx'}, dimensions={0} | all-to-all | bytes 4587520 | tf_op jit(solution)/shard_map/all_to_all | solution.py:81
  132.4 1.5 copy.143
  134.6 1.2 fusion.50
  137.6 1.0 iota_compare_fusion
  138.6 9.6 %fusion.5 = f32[2,1280,384]{1,2,0:T(8,128)} fusion(bf16[2,1792,384]{2,1,0:T(8,128)(2,1)S(1)} %copy-done, bf16[1,2,1280,1792]{3,2,1,0:T(8,128)(2,1)} %all-gather.5.cloned.1.call-done), kind=kOutput, calls=%fused_computation.7 | convolution fusion | flops 3523215360 | bytes 15859712 | tf_op jit(solution)/shard_map/prd,pdf->prf/dot_general | solution.py:11
  148.1 11.2 %fusion.13 = f32[2,1280,384]{1,2,0:T(8,128)} fusion(bf16[2,1792,384]{2,1,0:T(8,128)(2,1)S(1)} %copy-done.6, bf16[1,2,1280,1792]{3,2,1,0:T(8,128)(2,1)} %all-gather.5.cloned.1.call-done), kind=kOutput, calls=%fused_computation.15 | convolution fusion | flops 3524198400 | bytes 15859712 | tf_op jit(solution)/shard_map/prd,pdf->prf/dot_general | solution.py:12
  159.3 43.0 %all-gather.3.cloned.1.call-done = bf16[1,2,1280,1792]{3,2,1,0:T(8,128)(2,1)} async-done(((bf16[1,2,320,1792]{3,2,1,0:T(8,128)(2,1)}), bf16[1,2,1280,1792]{3,2,1,0:T(8,128)(2,1)}) %all-gather.3.cloned.1.call-update) | async-done | bytes 9175056 | tf_op jit(solution)/shard_map/all_gather | solution.py:92
  202.3 13.7 %multiply_reduce_fusion = (bf16[2,1280]{1,0:T(2,128)(2,1)}, bf16[2,1280,384]{1,2,0:T(8,128)(2,1)}, f32[2,1280,384]{1,2,0:T(8,128)}) fusion(f32[2,1280,384]{1,2,0:T(8,128)} %fusion.13, f32[2,1280,384]{1,2,0:T(8,128)} %fusion.5, bf16[2,384,1792]{2,1,0:T(8,128)(2,1)} %param.15, bf16[1,2,1280,1792]{3,2,1,0:T(8,128)(2,1)} %all-gather.3.cloned.1.call-done), kind=kOutput, calls=%fused_computation.16 | convolution fusion | flops 3533043200 | bytes 25695232 | tf_op jit(solution)/shard_map/prd,pfd->prf/dot_general | solution.py:15
  216.0 1.6 copy.173
  218.3 20.0 %reduce-scatter.8.cloned.1.call-done = bf16[320,2]{1,0:T(8,128)(2,1)} async-done(((bf16[1280,2]{1,0:T(8,128)(2,1)}), bf16[320,2]{1,0:T(8,128)(2,1)}) %reduce-scatter.8.cloned.1.call-update) | async-done | bytes 1296
  238.3 1.6 copy.152
  239.9 5.5 all-to-all-start.4
  246.2 2.1 eq.110
  248.3 3.6 all-to-all-done.4
  252.7 2.1 select_reduce_fusion
  254.8 0.9 copy.168
  255.7 1.9 multiply_reduce_fusion.1
  257.5 1.4 copy.139
  259.0 1.5 reshape.170
  260.5 1.9 fusion.23
  262.4 8.9 %all_to_all.74 = bf16[8,2,40]{2,1,0:T(2,128)(2,1)S(1)} all-to-all(bf16[8,2,40]{2,1,0:T(2,128)(2,1)S(1)} %convert_element_type.83), channel_id=1, replica_groups=mesh['dp'=4,'ctx'=8] {'ctx'}, dimensions={0} | all-to-all | bytes 2560 | tf_op jit(solution)/shard_map/all_to_all | solution.py:86
  271.9 1.3 all_to_all.55
  273.2 1.5 copy.141
  274.7 7.1 %all_gather.9 = bf16[1,2,1280]{1,0,2:T(2,128)(2,1)S(1)} all-gather(bf16[1,2,320]{1,0,2:T(2,128)(2,1)} %copy.141), channel_id=1, replica_groups=mesh['dp'=4,'ctx'=8] {'dp'}, dimensions={2}, use_global_device_ids=true | all-gather | bytes 6400 | tf_op jit(solution)/shard_map/all_gather | solution.py:93
  281.9 1.4 mul.155
  283.3 1.9 copy.142
  285.2 6.4 %multiply_convert_fusion.3 = (bf16[2,1280,384]{1,2,0:T(8,128)(2,1)}, bf16[2,1280,384]{1,2,0:T(8,128)(2,1)S(1)}) fusion(f32[2,1280,384]{1,2,0:T(8,128)} %fusion.5, f32[2,1280,384]{1,2,0:T(8,128)} %get-tuple-element.22, f32[2,1280]{1,0:T(2,128)} %copy.142, f32[2,1280,384]{1,2,0:T(8,128)} %fusion.13), kind=kLoop, calls=%fused_computation.18 | loop fusion | flops 14745600 | bytes 15738880 | tf_op jit(solution)/shard_map/convert_element_type | solution.py:20
  291.6 9.3 %fusion.53 = f32[2,1280,1792]{2,1,0:T(8,128)} fusion(bf16[2,1280,384]{1,2,0:T(8,128)(2,1)S(1)} %get-tuple-element.13, bf16[2,1792,384]{2,1,0:T(8,128)(2,1)S(1)} %copy-done), kind=kOutput, calls=%fused_computation.86 | convolution fusion | flops 3523215360 | bytes 23068672 | tf_op jit(solution)/shard_map/prf,pdf->prd/dot_general | solution.py:31
  301.0 16.4 %add_convert_fusion = bf16[2,1280,1792]{2,1,0:T(8,128)(2,1)} fusion(f32[2,1280,1792]{2,1,0:T(8,128)} %fusion.53, bf16[2,1280,384]{1,2,0:T(8,128)(2,1)} %get-tuple-element.12, bf16[2,1792,384]{2,1,0:T(8,128)(2,1)} %param.14), kind=kOutput, calls=%fused_computation.1 | convolution fusion | flops 3532390400 | bytes 32243712 | tf_op jit(solution)/shard_map/prf,pdf->prd/dot_general | solution.py:34
  317.4 73.7 %reduce-scatter.6.cloned.1.call-done = bf16[2,320,1792]{2,1,0:T(8,128)(2,1)} async-done(((bf16[2,1280,1792]{2,1,0:T(8,128)(2,1)}), bf16[2,320,1792]{2,1,0:T(8,128)(2,1)}) %reduce-scatter.6.cloned.1.call-update) | async-done | bytes 2293776 | tf_op jit(solution)/shard_map/reduce_scatter | solution.py:101
  391.1 5.4 copy.149
  396.5 5.7 all-to-all-start.3
  402.5 0.9 fusion.45
  403.5 12.0 %fusion.20 = bf16[2,1792,384]{2,1,0:T(8,128)(2,1)} fusion(bf16[2,1280,384]{1,2,0:T(8,128)(2,1)} %get-tuple-element.12, bf16[1,2,1280,1792]{3,2,1,0:T(8,128)(2,1)} %all-gather.5.cloned.1.call-done), kind=kOutput, calls=%fused_computation.23 | convolution fusion | flops 3524591616 | bytes 13893632 | tf_op jit(solution)/shard_map/prd,prf->pdf/dot_general | solution.py:28
  415.5 9.7 %fusion.16 = bf16[2,384,1792]{2,1,0:T(8,128)(2,1)} fusion(bf16[2,1280,384]{1,2,0:T(8,128)(2,1)} %get-tuple-element.11, bf16[1,2,1280,1792]{3,2,1,0:T(8,128)(2,1)} %all-gather.3.cloned.1.call-done, f32[2,1280]{1,0:T(2,128)S(1)} %copy-done.10), kind=kOutput, calls=%fused_computation.21 | convolution fusion | flops 3538354176 | bytes 13903872 | tf_op jit(solution)/shard_map/prf,prd->pfd/dot_general | solution.py:22
  425.2 12.3 %fusion.17 = bf16[2,1792,384]{2,1,0:T(8,128)(2,1)} fusion(bf16[2,1280,384]{1,2,0:T(8,128)(2,1)S(1)} %copy-done.3, bf16[1,2,1280,1792]{3,2,1,0:T(8,128)(2,1)} %all-gather.5.cloned.1.call-done), kind=kOutput, calls=%fused_computation.22 | convolution fusion | flops 3524591616 | bytes 13893632 | tf_op jit(solution)/shard_map/prd,prf->pdf/dot_general | solution.py:25
  437.5 111.5 %all-reduce.4.cloned.1.call-done = f32[1792,16]{0,1:T(8,128)} async-done(((f32[1792,16]{0,1:T(8,128)}), f32[1792,16]{0,1:T(8,128)}) %all-reduce.4.cloned.1.call-update) | async-done | bytes 114704
  548.9 1.4 constant_dynamic-slice_fusion
  550.8 1.4 fusion.54
  552.2 1.4 fusion.35
  553.5 41.1 %all-reduce.1 = f32[1792]{0:T(1024)S(1)} all-reduce(f32[1792]{0:T(1024)S(1)} %get-tuple-element.6), channel_id=5, replica_groups=mesh['dp'=4,'ctx'=8] {'dp','ctx'}, use_global_device_ids=true, to_apply=%region_15.16.clone | all-reduce | flops 1792 | bytes 14336
  595.2 2.5 fusion.34
  (88 shorter events, 9.7 us)
Async XLA Ops:
  7.2 131.4 %copy-start = (bf16[2,1792,384]{2,1,0:T(8,128)(2,1)S(1)}, bf16[2,1792,384]{2,1,0:T(8,128)(2,1)}, u32[]{:S(2)}) copy-start(bf16[2,1792,384]{2,1,0:T(8,128)(2,1)} %param.13) | copy-start | bytes 8257540
  7.2 131.4 %all-gather.5.cloned.1.call-start = ((), (), s32[]{:S(2)}) async-start(), calls=%async_computation.8 | async-start | bytes 11468800 | tf_op jit(solution)/shard_map/all_gather | solution.py:91
  9.6 64.4 %copy-start.16 = (f32[128]{0:T(128)}, f32[128]{0:T(128)S(1)}, u32[]{:S(2)}) copy-start(f32[128]{0:T(128)S(1)} %add_rsqrt_fusion) | copy-start | bytes 1540
  11.1 0.6 copy-start.12
  74.0 1.6 copy-start.7
  75.6 126.7 %all-gather.3.cloned.1.call-start = ((), (), s32[]{:S(2)}) async-start(), calls=%async_computation.7 | async-start | bytes 11468800 | tf_op jit(solution)/shard_map/all_gather | solution.py:92
  132.4 2.1 copy-start.4
  132.4 2.1 copy-start.8
  132.4 3.3 copy-start.11
  134.0 104.3 %reduce-scatter.8.cloned.1.call-start = ((), (), s32[]{:S(2)}) async-start(), calls=%async_computation.10 | async-start | bytes 409600
  137.0 0.5 copy-start.15
  138.5 9.6 %copy-start.6 = (bf16[2,1792,384]{2,1,0:T(8,128)(2,1)S(1)}, bf16[2,1792,384]{2,1,0:T(8,128)(2,1)}, u32[]{:S(2)}) copy-start(bf16[2,1792,384]{2,1,0:T(8,128)(2,1)} %param.14) | copy-start | bytes 8257540
  159.3 86.3 %copy-start.14 = (f32[128,4]{0,1:T(4,128)S(1)}, f32[128,4]{0,1:T(4,128)}, u32[]{:S(2)}) copy-start(f32[128,4]{0,1:T(4,128)} %select_reduce_fusion.2) | copy-start | bytes 6148
  239.9 12.0 %all-to-all-start.4 = ((bf16[2,8,40]{2,0,1:T(2,128)(2,1)}), bf16[2,8,40]{2,0,1:T(2,128)(2,1)}, u32[]{:S(2)}, u32[]{:S(2)}) async-start(bf16[2,8,40]{2,0,1:T(2,128)(2,1)} %copy.152), calls=%async_computation.5 | async-start | bytes 8192 | tf_op jit(solution)/shard_map/all_to_all | solution.py:112
  245.4 145.7 %reduce-scatter.6.cloned.1.call-start = ((), (), s32[]{:S(2)}) async-start(), calls=%async_computation.9 | async-start | bytes 11468800 | tf_op jit(solution)/shard_map/reduce_scatter | solution.py:101
  291.6 9.4 %copy-start.2 = (bf16[2,1280,384]{1,2,0:T(8,128)(2,1)}, bf16[2,1280,384]{1,2,0:T(8,128)(2,1)S(1)}, u32[]{:S(2)}) copy-start(bf16[2,1280,384]{1,2,0:T(8,128)(2,1)S(1)} %get-tuple-element.13) | copy-start | bytes 5898244
  396.5 6.0 copy-start.13
  396.5 6.0 copy-start.19
  396.5 6.0 copy-start.17
  396.5 153.9 %all-to-all-start.3 = ((bf16[2,320,1792]{2,0,1:T(2,128)(2,1)}), bf16[2,320,1792]{2,0,1:T(2,128)(2,1)S(1)}, u32[]{:S(2)}, u32[]{:S(2)}) async-start(bf16[2,320,1792]{2,0,1:T(2,128)(2,1)} %copy.149), calls=%async_computation.4 | async-start | bytes 4587520 | tf_op jit(solution)/shard_map/all_to_all | solution.py:109
  402.1 146.8 %all-reduce.4.cloned.1.call-start = ((), (), s32[]{:S(2)}) async-start(), calls=%async_computation.11 | async-start | bytes 229376
  403.5 12.0 %copy-start.10 = (f32[2,1280]{1,0:T(2,128)S(1)}, f32[2,1280]{1,0:T(2,128)}, u32[]{:S(2)}) copy-start(f32[2,1280]{1,0:T(2,128)} %copy.142) | copy-start | bytes 30724
  415.5 9.7 %copy-start.3 = (bf16[2,1280,384]{1,2,0:T(8,128)(2,1)S(1)}, bf16[2,1280,384]{1,2,0:T(8,128)(2,1)}, u32[]{:S(2)}) copy-start(bf16[2,1280,384]{1,2,0:T(8,128)(2,1)} %copy-done.2) | copy-start | bytes 5898244
  550.7 1.4 copy-start.5
  550.7 1.4 copy-start.9
  550.7 1.4 copy-start.18
  550.7 46.9 %copy-start.1 = (bf16[2,1792,384]{2,1,0:T(8,128)(2,1)S(1)}, bf16[2,1792,384]{2,1,0:T(8,128)(2,1)}, u32[]{:S(2)}) copy-start(bf16[2,1792,384]{2,1,0:T(8,128)(2,1)} %param.13) | copy-start | bytes 8257540
Sparse Core Ops, SparseCore 0:
  75.7 61.6 all-gather.4
  139.5 62.7 all-gather.2
  217.8 20.4 reduce-scatter.7
  317.5 73.4 reduce-scatter.5
  408.8 140.1 all-reduce.3
